TPU v7x, 512 devices: a whole 4x8x8 slice. The times are simulated.
512 devices in a mesh: seq: 64 (over z, x, y_hi), chan: 8 (over y_lo, core).
Axes of the slice: x: 4, y: 8 (y_hi: 2, y_lo: 4; y = y_hi * 4 + y_lo), z: 8, core: 2. Of those that a mesh axis runs over, the one named last changes fastest.
Arguments:
- values: bfloat16 [256, 32768], P('chan', 'seq'), may hold values from -6 to 6
- gate_one: bfloat16 [256, 32768], P('chan', 'seq'), may hold values from -6 to 6
- gate_two: bfloat16 [256, 32768], P('chan', 'seq'), may hold values from -6 to 6
- filter_one: float32 [256, 32768], P('chan', 'seq'), may hold values from -1 to 1
- filter_two: float32 [256, 32768], P('chan', 'seq'), may hold values from -1 to 1
- skip_one: float32 [256], P('chan'), may hold values from -1 to 1
- skip_two: float32 [256], P('chan'), may hold values from -1 to 1
- mix_weight: bfloat16 [256, 256], P(None, 'chan'), may hold values from -0.375 to 0.375
Outputs:
- mixed: bfloat16 [256, 32768], P('chan', 'seq')
All inputs are finite; a program needn't handle non-finite values.
Results may differ from a plain program's by a relative error of at most 0.0051.
Values may be sent and summed in bfloat16 or wider, within the bound.
No kernel may reach another device: no remote copies, remote signals or barrier semaphores. Data moves between devices by JAX's collectives and lax.ppermute only.
A program may use at most 64 MiB of HBM per device.

v0:
```python
import jax
import jax.numpy as jnp
from jax import lax
from jax.experimental import pallas as pl
from jax.experimental.pallas import tpu as pltpu
from jax.sharding import PartitionSpec as P

BLOCK = 128
PIECE = 64
SEQ_WAYS = 64
CHAN_WAYS = 8
OWN_CHANNELS = 32
OWN_BLOCKS = 4
ROWS = 20
BLOCKS = SEQ_WAYS * OWN_BLOCKS
LAGS = 128
SHIFTS = 8
PAD = 8
STEPS = 8
JOINED = 4
SPAN = SHIFTS * BLOCK
CHUNK = SPAN // PIECE
F32 = jnp.float32
BF16 = jnp.bfloat16


def swap(a):
    return pltpu.roll(a, PIECE, 1)


def join(low, high):
    return jnp.where(lax.broadcasted_iota(jnp.int32, low.shape, 1) < PIECE, low, high)


def pack_kernel(values, gate_one, gate_two, filter_one, filter_two, send, wide):
    for half in range(2):
        for kind, source in enumerate((values, filter_one, gate_one, filter_two, gate_two)):
            for q in range(OWN_BLOCKS):
                piece = source[:, q * BLOCK : (q + 1) * BLOCK].astype(F32)
                wide[pl.ds(half * ROWS + kind * OWN_BLOCKS + q, OWN_CHANNELS, stride=2 * ROWS), :] = piece
    send[...] = wide[...].astype(BF16)


def lay_taps(source, taps, turned, f):
    for c in range(2):
        top = PAD + 2 * c * LAGS // 2
        near = source[top : top + LAGS // 2, :]
        far = source[top + LAGS // 2 : top + LAGS, :]
        taps[2 * f + c, pl.ds(PAD, LAGS // 2, stride=2), :] = join(near, swap(far))
        taps[2 * f + c, pl.ds(PAD + 1, LAGS // 2, stride=2), :] = join(swap(near), far)
        last = source[top + LAGS // 2 - 1 : top + LAGS // 2, :]
        before = source[top - 1 : top, :]
        edge = join(swap(before), last)
        taps[2 * f + c, 0:PAD, :] = jnp.broadcast_to(edge, (PAD, BLOCK))
        turned[2 * f + c, 0 : PAD + LAGS, :] = swap(taps[2 * f + c, 0 : PAD + LAGS, :])
        for rows in (taps, turned):
            rows[2 * f + c, PAD + LAGS :, :] = jnp.zeros((CHUNK, BLOCK), F32)


def masks():
    lane = lax.broadcasted_iota(jnp.int32, (8, BLOCK), 1) % PIECE
    row = lax.broadcasted_iota(jnp.int32, (8, BLOCK), 0)
    return [lane < PIECE - 8 * m - row for m in range(PIECE // 8)]


def build_chunk(kept, taps, turned, f, lag, table, at, count=CHUNK):
    for k in range(count):
        for c in range(2):
            now = jnp.broadcast_to(taps[2 * f + c, pl.ds(lag + PAD + k, 1), :], (8, BLOCK))
            before = jnp.broadcast_to(turned[2 * f + c, pl.ds(lag + PAD + k - 1, 1), :], (8, BLOCK))
            tiles = [
                pltpu.roll(jnp.where(kept[m], now, before), 8 * m, 1, stride=1, stride_axis=0)
                for m in range(PIECE // 8)
            ]
            rows = pl.ds(at + k * PIECE, PIECE)
            table[rows, c * BLOCK : (c + 1) * BLOCK] = jnp.concatenate(tiles, axis=0).astype(BF16)


def side_by_side(pieces):
    return jnp.concatenate(pieces, axis=1)


def conv_kernel(
    skips, recv, out, wide, x_pad, h_one, h_two, gate, even, odd, taps, turned, x_wide, chunk_a, chunk_b, table_two, table_late,
    g_wide, acc, mixed, out_wide, spaced
):
    place = lax.axis_index("seq")
    half = place % 2
    tables_one = (chunk_a, chunk_b)
    channel = place // 2
    wide[...] = recv[...].astype(F32)
    for padded in (x_pad, h_one, h_two, even, odd):
        padded[0:PAD, :] = jnp.zeros((PAD, BLOCK), F32)
    x_wide[0 : 2 * PIECE, :] = jnp.zeros((2 * PIECE, SPAN), BF16)
    g_wide[:, 0:PIECE, :] = jnp.zeros((SHIFTS, PIECE, BLOCK), BF16)
    for q in range(OWN_BLOCKS):
        def rows_of(kind):
            return wide[pl.ds(kind * OWN_BLOCKS + q, SEQ_WAYS, stride=ROWS), :]
        x_pad[pl.ds(PAD + q, SEQ_WAYS, stride=OWN_BLOCKS), :] = rows_of(0)
        h_one[pl.ds(PAD + q, SEQ_WAYS, stride=OWN_BLOCKS), :] = rows_of(1)
        gate[pl.ds(q, SEQ_WAYS, stride=OWN_BLOCKS), :] = rows_of(2)
        h_two[pl.ds(PAD + q, SEQ_WAYS, stride=OWN_BLOCKS), :] = rows_of(3)

    lay_taps(h_one, taps, turned, 0)
    lay_taps(h_two, taps, turned, 1)
    kept = masks()
    build_chunk(kept, taps, turned, 0, 0, tables_one[0], 0)

    x_now = x_pad[PAD : PAD + BLOCKS, :]
    even[PAD : PAD + BLOCKS, :] = join(x_now, x_pad[PAD - 1 : PAD - 1 + BLOCKS, :])
    odd[PAD : PAD + BLOCKS, :] = swap(x_now)
    groups = BLOCKS // 8
    for b in range(SHIFTS):
        stacked = jnp.concatenate(
            [
                even[PAD - b : PAD - b + BLOCKS, :].reshape(groups, 8, BLOCK),
                odd[PAD - b : PAD - b + BLOCKS, :].reshape(groups, 8, BLOCK),
            ],
            axis=1,
        )
        x_wide[2 * PIECE : 2 * PIECE + 2 * BLOCKS, b * BLOCK : (b + 1) * BLOCK] = stacked.reshape(
            2 * BLOCKS, BLOCK
        ).astype(BF16)

    acc[...] = jnp.zeros((2 * BLOCKS, 2 * BLOCK), F32)

    def first_conv(i, carry):
        total = acc[...]
        for j in range(JOINED):
            a = i * JOINED + j
            total += jnp.dot(
                x_wide[pl.ds(pl.multiple_of(2 * PIECE - 16 * a, 16), 2 * BLOCKS), :],
                tables_one[j % 2][...],
                preferred_element_type=F32,
            )
            build_chunk(kept, taps, turned, 0, (a + 1) * CHUNK, tables_one[(j + 1) % 2], 0)
            at = pl.multiple_of(a * (SPAN // 2), SPAN // 2)
            build_chunk(kept, taps, turned, 1, a * (CHUNK // 2), table_two, at, CHUNK // 2)
        acc[...] = total
        return carry

    lax.fori_loop(0, STEPS // JOINED, first_conv, 0)

    def group(n, parity):
        at = 16 * n + 8 * parity
        total = acc[at : at + 8, 0:BLOCK]
        if n >= groups // 2:
            back = at - BLOCKS
            total = total + acc[back : back + 8, BLOCK : 2 * BLOCK]
        return total

    first_skip = skips[pl.ds(channel, 1), :]
    second_skip = skips[pl.ds(OWN_CHANNELS + channel, 1), :]
    is_odd = half == 1
    spaced[0 : 2 * PAD, :] = jnp.zeros((2 * PAD, BLOCK), F32)
    start = pl.multiple_of(2 * PAD - 8 * half, 8)
    for n in range(groups):
        here = [group(n, parity) for parity in range(2)]
        rows = slice(8 * n, 8 * n + 8)
        padded_rows = slice(PAD + 8 * n, PAD + 8 * n + 8)
        if n >= groups // 4:
            prior = [group(n - groups // 4, parity) for parity in range(2)]
        else:
            prior = [jnp.zeros((8, BLOCK), F32)] * 2
        conv_one = join(here[0], prior[1]) + swap(join(here[1], prior[0]))
        h_one[padded_rows, :] = gate[rows, :] * (conv_one + first_skip * x_pad[padded_rows, :])
    gated = h_one[PAD : PAD + BLOCKS, :]
    even[0:BLOCKS, :] = join(gated, h_one[PAD - 1 : PAD - 1 + BLOCKS, :])
    odd[0:BLOCKS, :] = swap(gated)
    for n in range(groups):
        spaced[pl.ds(start + 16 * n, 8, stride=2), :] = even[8 * n : 8 * n + 8, :]
        spaced[pl.ds(start + 16 * n + 1, 8, stride=2), :] = odd[8 * n : 8 * n + 8, :]
    for b in range(SHIFTS):
        picked = [spaced[2 * PAD + 16 * n - 2 * b : 2 * PAD + 16 * n - 2 * b + 8, :] for n in range(groups)]
        if b == 0:
            even[0:BLOCKS, :] = jnp.concatenate(picked, axis=0)
        g_wide[b, PIECE : PIECE + BLOCKS, :] = jnp.concatenate(picked, axis=0).astype(BF16)
    total = None
    for a in range(STEPS):
        early = a < STEPS // 2
        at = (a % (STEPS // 2)) * SPAN
        part = jnp.dot(
            side_by_side([g_wide[b, PIECE - 8 * a : PIECE - 8 * a + BLOCKS, :] for b in range(SHIFTS)]),
            (table_two if early else table_late)[at : at + SPAN, :],
            preferred_element_type=F32,
        )
        if early:
            build_chunk(kept, taps, turned, 1, LAGS // 2 + a * CHUNK, table_late, at)
        total = part if a == 0 else total + part
        if a == STEPS // 2 - 1 or a == STEPS - 1:
            acc[0:BLOCKS, :] = total
            total = acc[0:BLOCKS, :]

    mixed[0:LAGS, :] = acc[0:LAGS, 0:BLOCK]
    mixed[LAGS:BLOCKS, :] = acc[LAGS:BLOCKS, 0:BLOCK] + acc[0:LAGS, BLOCK : 2 * BLOCK]
    gate[0:PIECE, :] = mixed[0:PIECE, :] + second_skip * even[0:PIECE, :]
    gate[PIECE:BLOCKS, :] = (
        mixed[PIECE:BLOCKS, :] + swap(mixed[0 : BLOCKS - PIECE, :]) + second_skip * even[PIECE:BLOCKS, :]
    )
    for u in range(OWN_BLOCKS):
        low = gate[pl.ds(2 * u, OWN_CHANNELS, stride=8), :]
        high = gate[pl.ds(2 * u + 1, OWN_CHANNELS, stride=8), :]
        gates = [wide[pl.ds(p * ROWS + 4 * OWN_BLOCKS + u, OWN_CHANNELS, stride=2 * ROWS), :] for p in range(2)]
        result = jnp.where(is_odd, gates[1], gates[0]) * join(low, swap(high))
        for copy in range(2):
            out_wide[pl.ds(OWN_BLOCKS * copy + u, OWN_CHANNELS, stride=2 * OWN_BLOCKS), :] = result
    for n in range(OWN_CHANNELS):
        once = out_wide[8 * n : 8 * n + 8, :]
        twice = jnp.concatenate([once, once], axis=0).astype(BF16)
        for copy in range(2):
            out[32 * n + 16 * copy : 32 * n + 16 * copy + 16, :] = twice


def side_kernel(weight, skip_one, skip_two, out, skips, spread):
    square = (OWN_CHANNELS, OWN_CHANNELS)
    same = lax.broadcasted_iota(jnp.int32, square, 0) == lax.broadcasted_iota(jnp.int32, square, 1)
    for i, skip in enumerate((skip_one, skip_two)):
        column = jnp.sum(jnp.where(same, jnp.broadcast_to(skip[...], square), 0.0), axis=1, keepdims=True)
        skips[i * OWN_CHANNELS : (i + 1) * OWN_CHANNELS, :] = jnp.broadcast_to(column, (OWN_CHANNELS, BLOCK))
    quarter = lax.broadcasted_iota(jnp.int32, (OWN_CHANNELS, BLOCK), 1) // OWN_CHANNELS
    for c in range(CHAN_WAYS):
        own = weight[c * OWN_CHANNELS : (c + 1) * OWN_CHANNELS, :].astype(F32)
        repeated = jnp.concatenate([own] * OWN_BLOCKS, axis=1)
        for u in range(OWN_BLOCKS):
            spread[pl.ds(OWN_BLOCKS * c + u, OWN_CHANNELS, stride=OWN_BLOCKS * CHAN_WAYS), :] = jnp.where(
                quarter == u, repeated, 0.0
            )
    out[...] = spread[...].astype(BF16)


def mix_kernel(weight, recv, out):
    summed = lax.dot_general(weight[...], recv[...], (((0,), (0,)), ((), ())), preferred_element_type=F32)
    active = (summed / (1.0 + jnp.exp(-summed))).astype(BF16)
    for u in range(OWN_BLOCKS):
        out[:, u * BLOCK : (u + 1) * BLOCK] = active[u * OWN_CHANNELS : (u + 1) * OWN_CHANNELS, :]


def per_device(values, gate_one, gate_two, filter_one, filter_two, skip_one, skip_two, mix_weight):
    whole = pl.BlockSpec(memory_space=pltpu.VMEM)
    send = pl.pallas_call(
        pack_kernel,
        out_shape=jax.ShapeDtypeStruct((SEQ_WAYS * ROWS, BLOCK), BF16),
        in_specs=[whole] * 5,
        out_specs=whole,
        scratch_shapes=[pltpu.VMEM((SEQ_WAYS * ROWS, BLOCK), F32)],
        name="pack",
    )(values, gate_one, gate_two, filter_one, filter_two)
    recv = lax.all_to_all(
        send.reshape(SEQ_WAYS, ROWS // 2, 2, BLOCK), "seq", split_axis=0, concat_axis=0, tiled=True
    ).reshape(SEQ_WAYS * ROWS, BLOCK)
    laid_weight, skips = pl.pallas_call(
        side_kernel,
        out_shape=(
            jax.ShapeDtypeStruct((OWN_CHANNELS * CHAN_WAYS * OWN_BLOCKS, BLOCK), BF16),
            jax.ShapeDtypeStruct((2 * OWN_CHANNELS, BLOCK), F32),
        ),
        in_specs=[whole] * 3,
        out_specs=(whole, whole),
        scratch_shapes=[pltpu.VMEM((OWN_CHANNELS * CHAN_WAYS * OWN_BLOCKS, BLOCK), F32)],
        compiler_params=pltpu.CompilerParams(vmem_limit_bytes=8 << 20),
        name="side",
    )(mix_weight, skip_one.reshape(1, OWN_CHANNELS), skip_two.reshape(1, OWN_CHANNELS))
    spread = pl.pallas_call(
        conv_kernel,
        out_shape=jax.ShapeDtypeStruct((SEQ_WAYS * CHAN_WAYS * 2, BLOCK), BF16),
        in_specs=[whole, whole],
        out_specs=whole,
        scratch_shapes=[
            pltpu.VMEM((SEQ_WAYS * ROWS, BLOCK), F32),
            pltpu.VMEM((PAD + BLOCKS, BLOCK), F32),
            pltpu.VMEM((PAD + BLOCKS, BLOCK), F32),
            pltpu.VMEM((PAD + BLOCKS, BLOCK), F32),
            pltpu.VMEM((BLOCKS, BLOCK), F32),
            pltpu.VMEM((PAD + BLOCKS, BLOCK), F32),
            pltpu.VMEM((PAD + BLOCKS, BLOCK), F32),
            pltpu.VMEM((4, PAD + LAGS + CHUNK, BLOCK), F32),
            pltpu.VMEM((4, PAD + LAGS + CHUNK, BLOCK), F32),
            pltpu.VMEM((2 * PIECE + 2 * BLOCKS, SPAN), BF16),
            pltpu.VMEM((SPAN, 2 * BLOCK), BF16),
            pltpu.VMEM((SPAN, 2 * BLOCK), BF16),
            pltpu.VMEM((LAGS // 2 * PIECE, 2 * BLOCK), BF16),
            pltpu.VMEM((LAGS // 2 * PIECE, 2 * BLOCK), BF16),
            pltpu.VMEM((SHIFTS, PIECE + BLOCKS, BLOCK), BF16),
            pltpu.VMEM((2 * BLOCKS, 2 * BLOCK), F32),
            pltpu.VMEM((BLOCKS, BLOCK), F32),
            pltpu.VMEM((BLOCKS, BLOCK), F32),
            pltpu.VMEM((2 * PAD + 2 * BLOCKS, BLOCK), F32),
        ],
        compiler_params=pltpu.CompilerParams(vmem_limit_bytes=32 << 20),
        name="convs",
    )(skips, recv)
    gathered = lax.all_to_all(
        spread.reshape(OWN_CHANNELS * CHAN_WAYS, OWN_BLOCKS // 2, 2, BLOCK),
        ("seq", "chan"),
        split_axis=0,
        concat_axis=0,
        tiled=True,
        axis_index_groups=[
            [(2 * k + half) * CHAN_WAYS + c for k in range(OWN_CHANNELS) for c in range(CHAN_WAYS)] for half in range(2)
        ],
    ).reshape(SEQ_WAYS * CHAN_WAYS * 2, BLOCK)
    return pl.pallas_call(
        mix_kernel,
        out_shape=jax.ShapeDtypeStruct((OWN_CHANNELS, OWN_BLOCKS * BLOCK), BF16),
        in_specs=[whole, whole],
        out_specs=whole,
        compiler_params=pltpu.CompilerParams(vmem_limit_bytes=8 << 20),
        name="mix",
    )(laid_weight, gathered)


def solution(mesh):
    return jax.shard_map(
        per_device,
        mesh=mesh,
        in_specs=(
            P("chan", "seq"),
            P("chan", "seq"),
            P("chan", "seq"),
            P("chan", "seq"),
            P("chan", "seq"),
            P("chan"),
            P("chan"),
            P(None, "chan"),
        ),
        out_specs=P("chan", "seq"),
        check_vma=False,
    )
```

profile of v0, /device:TPU:1, one launch (start us, length us, event | category | flops | bytes accessed | tf_op | source)
XLA Modules:
  0.0 69.3 jit_solution(15422448205262607032)
XLA Ops:
  0.0 1.8 %pack.1 = bf16[1280,128]{1,0:T(8,128)(2,1)} custom-call(bf16[32,512]{1,0:T(8,128)(2,1)} %values.1, bf16[32,512]{1,0:T(8,128)(2,1)} %gate_one.1, bf16[32,512]{1,0:T(8,128)(2,1)} %gate_two.1, f32[32,512]{1,0:T(8,128)} %filter_one.1, f32[32,512]{1,0:T(8,128)} %filter_two.1), custom_call_target="tpu_custom_call" | custom-call | tf_op jit(solution)/shard_map/pack/pallas_call | solution.py:240
  1.8 0.0 copy-start.2
  1.8 19.7 %all-to-all-start = ((bf16[64,10,2,128]{3,2,1,0:T(2,128)(2,1)}), bf16[64,10,2,128]{3,2,1,0:T(2,128)(2,1)S(1)}, u32[]{:S(2)}, u32[]{:S(2)}) async-start(bf16[64,10,2,128]{3,2,1,0:T(2,128)(2,1)} %bitcast.11), calls=%async_computation | async-start | bytes 655360 | tf_op jit(solution)/shard_map/all_to_all | solution.py:248
  21.5 0.0 copy-done.2
  21.5 0.1 copy.9.weight
  21.6 0.0 copy-start
  21.6 0.0 copy-start.1
  21.7 0.6 copy-done
  22.3 0.0 copy-done.1
  22.3 0.5 side.1
  22.8 13.2 %all-to-all-done = bf16[64,10,2,128]{3,2,1,0:T(2,128)(2,1)S(1)} async-done(((bf16[64,10,2,128]{3,2,1,0:T(2,128)(2,1)}), bf16[64,10,2,128]{3,2,1,0:T(2,128)(2,1)S(1)}, u32[]{:S(2)}, u32[]{:S(2)}) %all-to-all-start) | async-done | bytes 327712 | tf_op jit(solution)/shard_map/all_to_all | solution.py:248
  36.0 5.7 %convs.1 = bf16[1024,128]{1,0:T(8,128)(2,1)S(1)} custom-call(f32[64,128]{1,0:T(8,128)S(1)} %get-tuple-element.8.skips, bf16[1280,128]{1,0:T(8,128)(2,1)S(1)} %bitcast.6), custom_call_target="tpu_custom_call" | custom-call | tf_op jit(solution)/shard_map/convs/pallas_call | solution.py:263
  41.7 26.7 %all_to_all.10 = bf16[256,2,2,128]{3,2,1,0:T(2,128)(2,1)S(1)} all-to-all(bf16[256,2,2,128]{3,2,1,0:T(2,128)(2,1)S(1)} %bitcast.8), channel_id=1, replica_groups={{0,1,2,3,4,5,6,7,16,17,18,19,20,21,22,23,32,33,34,35,36,37,38,39,48,49,..., dimensions={0} | all-to-all | bytes 524288 | tf_op jit(solution)/shard_map/all_to_all | solution.py:292
  68.4 0.9 %mix.1 = bf16[32,512]{1,0:T(8,128)(2,1)} custom-call(bf16[1024,128]{1,0:T(8,128)(2,1)S(1)} %get-tuple-element.7.weight, bf16[1024,128]{1,0:T(8,128)(2,1)S(1)} %bitcast.7), custom_call_target="tpu_custom_call" | custom-call | tf_op jit(solution)/shard_map/mix/pallas_call | solution.py:302
Async XLA Ops:
  1.8 19.7 %copy-start.2 = (bf16[256,32]{0,1:T(8,128)(2,1)S(1)}, bf16[256,32]{0,1:T(8,128)(2,1)}, u32[]{:S(2)}) copy-start(bf16[256,32]{0,1:T(8,128)(2,1)} %param.15) | copy-start | bytes 49156
  1.8 34.2 %all-to-all-start = ((bf16[64,10,2,128]{3,2,1,0:T(2,128)(2,1)}), bf16[64,10,2,128]{3,2,1,0:T(2,128)(2,1)S(1)}, u32[]{:S(2)}, u32[]{:S(2)}) async-start(bf16[64,10,2,128]{3,2,1,0:T(2,128)(2,1)} %bitcast.11), calls=%async_computation | async-start | bytes 655360 | tf_op jit(solution)/shard_map/all_to_all | solution.py:248
  21.6 0.7 copy-start
  21.6 0.7 copy-start.1
where the time goes:
time: 69.6 us; the launch traced here: 69.3 us
  blocking collectives  26.7 us (38%)
  starting transfers between devices  19.7 us (28%)
  waiting for transfers between devices  13.2 us (19%)
  Pallas kernels  8.88 us (13%)
  local copies, waits for them, and re-layouts  0.78 us (1%)
    all_to_all x1, blocking collectives, per_device(): lax.all_to_all(spread.reshape(OWN_CHANNELS * CHAN_WAYS, OWN_BLOCKS // 2,...  26.7 us
    all_to_all x1, starting transfers between devices, per_device(): lax.all_to_all(send.reshape(SEQ_WAYS, ROWS // 2, 2, BLOCK), 'seq', split_...  19.7 us
    all_to_all x1, waiting for transfers between devices, per_device(): lax.all_to_all(send.reshape(SEQ_WAYS, ROWS // 2, 2, BLOCK), 'seq', split_...  13.2 us
    pallas_call x1, Pallas kernels, per_device(): pl.pallas_call(conv_kernel, out_shape=jax.ShapeDtypeStruct((SEQ_WAYS * CH...  5.68 us
    pallas_call x1, Pallas kernels, per_device(): pl.pallas_call(pack_kernel, out_shape=jax.ShapeDtypeStruct((SEQ_WAYS * RO...  1.78 us
  transfers between devices with their start and end apart: 1, of which 1 were waited for; matrix products, arithmetic and copies ran while one was open for 0% of the time, Pallas kernels for 1%

commit v1 on v0

--- a/solution.py
+++ b/solution.py
@@ -32,13 +32,32 @@
     return jnp.where(lax.broadcasted_iota(jnp.int32, low.shape, 1) < PIECE, low, high)
 
 
-def pack_kernel(values, gate_one, gate_two, filter_one, filter_two, send, wide):
-    for half in range(2):
-        for kind, source in enumerate((values, filter_one, gate_one, filter_two, gate_two)):
-            for q in range(OWN_BLOCKS):
-                piece = source[:, q * BLOCK : (q + 1) * BLOCK].astype(F32)
+def pack_kernel(values, gate_one, gate_two, filter_one, filter_two, send, wide, narrow, broad, ready, arrived, left):
+    places = (
+        (filter_one, broad.at[0], 1),
+        (filter_two, broad.at[1], 3),
+        (values, narrow.at[0], 0),
+        (gate_one, narrow.at[1], 2),
+        (gate_two, narrow.at[2], 4),
+    )
+    fetches = [pltpu.make_async_copy(source, local, arrived.at[i]) for i, (source, local, _) in enumerate(places)]
+    for fetch in fetches:
+        fetch.start()
+    for fetch, (_, local, kind) in zip(fetches, places):
+        fetch.wait()
+        for q in range(OWN_BLOCKS):
+            piece = local[:, q * BLOCK : (q + 1) * BLOCK].astype(F32)
+            for half in range(2):
                 wide[pl.ds(half * ROWS + kind * OWN_BLOCKS + q, OWN_CHANNELS, stride=2 * ROWS), :] = piece
-    send[...] = wide[...].astype(BF16)
+    part = SEQ_WAYS * ROWS // 2
+    sends = []
+    for i in range(2):
+        rows = pl.ds(i * part, part)
+        ready[rows, :] = wide[rows, :].astype(BF16)
+        sends.append(pltpu.make_async_copy(ready.at[rows], send.at[rows], left.at[i]))
+        sends[i].start()
+    for one in sends:
+        one.wait()
 
 
 def lay_taps(source, taps, turned, f):
@@ -237,12 +256,20 @@
 
 def per_device(values, gate_one, gate_two, filter_one, filter_two, skip_one, skip_two, mix_weight):
     whole = pl.BlockSpec(memory_space=pltpu.VMEM)
+    outside = pl.BlockSpec(memory_space=pl.ANY)
     send = pl.pallas_call(
         pack_kernel,
         out_shape=jax.ShapeDtypeStruct((SEQ_WAYS * ROWS, BLOCK), BF16),
-        in_specs=[whole] * 5,
-        out_specs=whole,
-        scratch_shapes=[pltpu.VMEM((SEQ_WAYS * ROWS, BLOCK), F32)],
+        in_specs=[outside] * 5,
+        out_specs=outside,
+        scratch_shapes=[
+            pltpu.VMEM((SEQ_WAYS * ROWS, BLOCK), F32),
+            pltpu.VMEM((3, OWN_CHANNELS, OWN_BLOCKS * BLOCK), BF16),
+            pltpu.VMEM((2, OWN_CHANNELS, OWN_BLOCKS * BLOCK), F32),
+            pltpu.VMEM((SEQ_WAYS * ROWS, BLOCK), BF16),
+            pltpu.SemaphoreType.DMA((5,)),
+            pltpu.SemaphoreType.DMA((2,)),
+        ],
         name="pack",
     )(values, gate_one, gate_two, filter_one, filter_two)
     recv = lax.all_to_all(

time: 69.6 us -> 69.4 us (level)
  no operation moved by 1% of the time
where the time goes in v1:
time: 69.4 us; the launch traced here: 69.1 us
  blocking collectives  26.7 us (38%)
  starting transfers between devices  19.6 us (28%)
  waiting for transfers between devices  13.2 us (19%)
  Pallas kernels  8.85 us (13%)
  local copies, waits for them, and re-layouts  0.78 us (1%)
    all_to_all x1, blocking collectives, per_device(): lax.all_to_all(spread.reshape(OWN_CHANNELS * CHAN_WAYS, OWN_BLOCKS // 2,...  26.7 us
    all_to_all x1, starting transfers between devices, per_device(): lax.all_to_all(send.reshape(SEQ_WAYS, ROWS // 2, 2, BLOCK), 'seq', split_...  19.6 us
    all_to_all x1, waiting for transfers between devices, per_device(): lax.all_to_all(send.reshape(SEQ_WAYS, ROWS // 2, 2, BLOCK), 'seq', split_...  13.2 us
    pallas_call x1, Pallas kernels, per_device(): pl.pallas_call(conv_kernel, out_shape=jax.ShapeDtypeStruct((SEQ_WAYS * CH...  5.68 us
    pallas_call x1, Pallas kernels, per_device(): pl.pallas_call(pack_kernel, out_shape=jax.ShapeDtypeStruct((SEQ_WAYS * RO...  1.75 us
  transfers between devices with their start and end apart: 1, of which 1 were waited for; matrix products, arithmetic and copies ran while one was open for 0% of the time, Pallas kernels for 1%

profile of v1, /device:TPU:1, one launch (start us, length us, event | category | flops | bytes accessed | tf_op | source)
XLA Modules:
  0.0 69.1 jit_solution(15106200934887801986)
XLA Ops:
  0.0 1.8 %pack.1 = bf16[1280,128]{1,0:T(8,128)(2,1)} custom-call(bf16[32,512]{1,0:T(8,128)(2,1)} %values.1, bf16[32,512]{1,0:T(8,128)(2,1)} %gate_one.1, bf16[32,512]{1,0:T(8,128)(2,1)} %gate_two.1, f32[32,512]{1,0:T(8,128)} %filter_one.1, f32[32,512]{1,0:T(8,128)} %filter_two.1), custom_call_target="tpu_custom_call" | custom-call | tf_op jit(solution)/shard_map/pack/pallas_call | solution.py:260
  1.8 0.0 copy-start.2
  1.8 19.6 %all-to-all-start = ((bf16[64,10,2,128]{3,2,1,0:T(2,128)(2,1)}), bf16[64,10,2,128]{3,2,1,0:T(2,128)(2,1)S(1)}, u32[]{:S(2)}, u32[]{:S(2)}) async-start(bf16[64,10,2,128]{3,2,1,0:T(2,128)(2,1)} %bitcast.11), calls=%async_computation | async-start | bytes 655360 | tf_op jit(solution)/shard_map/all_to_all | solution.py:275
  21.4 0.0 copy-done.2
  21.4 0.1 copy.9.weight
  21.5 0.0 copy-start
  21.5 0.0 copy-start.1
  21.5 0.6 copy-done
  22.2 0.0 copy-done.1
  22.2 0.5 side.1
  22.7 13.2 %all-to-all-done = bf16[64,10,2,128]{3,2,1,0:T(2,128)(2,1)S(1)} async-done(((bf16[64,10,2,128]{3,2,1,0:T(2,128)(2,1)}), bf16[64,10,2,128]{3,2,1,0:T(2,128)(2,1)S(1)}, u32[]{:S(2)}, u32[]{:S(2)}) %all-to-all-start) | async-done | bytes 327712 | tf_op jit(solution)/shard_map/all_to_all | solution.py:275
  35.9 5.7 %convs.1 = bf16[1024,128]{1,0:T(8,128)(2,1)S(1)} custom-call(f32[64,128]{1,0:T(8,128)S(1)} %get-tuple-element.8.skips, bf16[1280,128]{1,0:T(8,128)(2,1)S(1)} %bitcast.6), custom_call_target="tpu_custom_call" | custom-call | tf_op jit(solution)/shard_map/convs/pallas_call | solution.py:290
  41.5 26.7 %all_to_all.10 = bf16[256,2,2,128]{3,2,1,0:T(2,128)(2,1)S(1)} all-to-all(bf16[256,2,2,128]{3,2,1,0:T(2,128)(2,1)S(1)} %bitcast.8), channel_id=1, replica_groups={{0,1,2,3,4,5,6,7,16,17,18,19,20,21,22,23,32,33,34,35,36,37,38,39,48,49,..., dimensions={0} | all-to-all | bytes 524288 | tf_op jit(solution)/shard_map/all_to_all | solution.py:319
  68.2 0.9 %mix.1 = bf16[32,512]{1,0:T(8,128)(2,1)} custom-call(bf16[1024,128]{1,0:T(8,128)(2,1)S(1)} %get-tuple-element.7.weight, bf16[1024,128]{1,0:T(8,128)(2,1)S(1)} %bitcast.7), custom_call_target="tpu_custom_call" | custom-call | tf_op jit(solution)/shard_map/mix/pallas_call | solution.py:329
Async XLA Ops:
  1.8 19.6 %copy-start.2 = (bf16[256,32]{0,1:T(8,128)(2,1)S(1)}, bf16[256,32]{0,1:T(8,128)(2,1)}, u32[]{:S(2)}) copy-start(bf16[256,32]{0,1:T(8,128)(2,1)} %param.15) | copy-start | bytes 49156
  1.8 34.1 %all-to-all-start = ((bf16[64,10,2,128]{3,2,1,0:T(2,128)(2,1)}), bf16[64,10,2,128]{3,2,1,0:T(2,128)(2,1)S(1)}, u32[]{:S(2)}, u32[]{:S(2)}) async-start(bf16[64,10,2,128]{3,2,1,0:T(2,128)(2,1)} %bitcast.11), calls=%async_computation | async-start | bytes 655360 | tf_op jit(solution)/shard_map/all_to_all | solution.py:275
  21.5 0.7 copy-start
  21.5 0.7 copy-start.1
